TPU v7x, 32 devices: a whole 2x2x4 slice. The times are simulated.
32 devices in a mesh: chan: 8 (over y, x, core), tm: 4 (over z).
Axes of the slice: x: 2, y: 2, z: 4, core: 2. Of those that a mesh axis runs over, the one named last changes fastest.
Arguments:
- voltages: bfloat16 [2, 8, 2048, 512], P(None, None, 'chan', 'tm'), may hold values from -0.25 to 0.25
- assignment: int32 [1024, 1], replicated, may hold values from 0 to 7; in each aligned block of 1024 rows (0 to 1023, 1024 to 2047, ...) at most 192 rows name the same one
- slot_subarray_index: int32 [8], replicated, may hold values from 0 to 7, each once
Outputs:
- visibilities: float32 [8, 8, 2, 384, 384], P('tm', 'chan')
Inputs may be any that keep to these rules, and one draw needn't show every extreme that they name: `assignment`: no subarray holds more than 192 antennas; one holds exactly 192. `slot_subarray_index`: each subarray appears once.
All inputs are finite; a program needn't handle non-finite values.
Results may differ from a plain program's by a relative error of at most 0.008.
Values may be sent and summed in bfloat16 or wider, within the bound.
A program may use at most 64 MiB of HBM per device.

v0:
```python
import jax
import jax.numpy as jnp
from jax import lax
from jax.sharding import PartitionSpec as P

SLOT = 384


def result_slot_lookup(assignment, slot_subarray_index, subarrays, slots, inputs):
    owner = jnp.repeat(assignment[:, 0], 2)
    onehot = (owner[:, None] == jnp.arange(subarrays, dtype=jnp.int32)[None, :]).astype(jnp.int32)
    ranks = jnp.sum((jnp.cumsum(onehot, axis=0) - onehot) * onehot, axis=1)
    table = jnp.full((subarrays, slots), inputs, jnp.int32)
    table = table.at[owner, ranks].set(jnp.arange(inputs, dtype=jnp.int32))
    return table[slot_subarray_index].reshape(-1)


def compact(block, rows, subarrays, slots):
    parts, chans, inputs, samples = block.shape
    padded_voltages = jnp.concatenate(
        [block, jnp.zeros((parts, chans, 1, samples), block.dtype)], axis=2
    )
    picked = jnp.take(padded_voltages, rows, axis=2)
    picked = picked.reshape(parts, chans, subarrays, slots, samples)
    picked = jnp.transpose(picked, (2, 1, 0, 3, 4))
    return picked.reshape(subarrays, chans, 2 * slots, samples)


def gram(stacked):
    full = jnp.einsum("...pt,...qt->...pq", stacked, stacked, preferred_element_type=jnp.float32)
    half = stacked.shape[-2] // 2
    real = full[..., :half, :half] + full[..., half:, half:]
    imag = full[..., half:, :half] - full[..., :half, half:]
    return jnp.stack([real, imag], axis=-3)


def shards(voltages, assignment, slot_subarray_index):
    subarrays = slot_subarray_index.shape[0]
    slots = SLOT
    inputs = 2 * assignment.shape[0]
    rows = result_slot_lookup(assignment, slot_subarray_index, subarrays, slots, inputs)
    local_samples = voltages.shape[3]
    time_groups = lax.axis_size("tm")
    stacked = compact(
        lax.all_to_all(voltages, "chan", split_axis=1, concat_axis=2, tiled=True),
        rows,
        subarrays,
        slots,
    )
    received = lax.all_to_all(stacked, "tm", split_axis=0, concat_axis=3, tiled=True)
    total = None
    for block_index in range(time_groups):
        piece = received[..., block_index * local_samples : (block_index + 1) * local_samples]
        rounded = gram(piece).astype(jnp.bfloat16).astype(jnp.float32)
        total = rounded if total is None else total + rounded
    return total


def solution(mesh):
    placed = (P(None, None, "chan", "tm"), P(), P())
    return jax.shard_map(
        shards,
        mesh=mesh,
        in_specs=placed,
        out_specs=P("tm", "chan", None, None, None),
        check_vma=False,
    )
```

profile of v0, /device:TPU:0, one launch (start us, length us, event | category | flops | bytes accessed | tf_op | source)
XLA Modules:
  0.0 84.1 jit_solution(1011175587574448796)
XLA Ops:
  0.0 2.3 %copy.13 = bf16[2,8,256,128]{3,2,0,1:T(8,128)(2,1)} copy(bf16[2,8,256,128]{3,2,1,0:T(8,128)(2,1)} %param.3) | data formatting | bytes 2097152 | tf_op args[0]
  2.3 0.0 copy-start
  2.3 0.0 copy-start.3
  2.3 5.3 %all-to-all-start = ((bf16[2,8,256,128]{3,2,0,1:T(8,128)(2,1)}), bf16[2,8,256,128]{3,2,0,1:T(8,128)(2,1)S(1)}, u32[]{:S(2)}, u32[]{:S(2)}) async-start(bf16[2,8,256,128]{3,2,0,1:T(8,128)(2,1)} %copy.13), calls=%async_computation | async-start | bytes 2097152 | tf_op jit(solution)/shard_map/all_to_all | solution.py:45
  7.6 0.0 copy-start.2
  7.6 0.0 copy-start.1
  7.6 0.0 copy-done
  7.7 0.2 broadcast_in_dim.30
  7.9 0.3 eq.23
  8.1 0.3 reshape.321
  8.4 0.0 copy-done.3
  8.5 0.6 broadcast.137
  9.1 0.7 reduce.9
  9.8 0.1 broadcast_in_dim.31
  9.9 0.1 copy.11
  10.0 0.1 copy.12
  10.0 2.3 %reduce-window.6 = s32[8,16,128]{2,1,0:T(8,128)S(1)} reduce-window(s32[8,16,128]{2,1,0:T(8,128)S(1)} %fusion.19, s32[]{:T(128)} %constant.11.clone.1), window={size=1x1x128 pad=0_0x0_0x127_0}, to_apply=%region_0.0 | reduce-window | flops 2080768 | bytes 131076 | tf_op jit(solution)/shard_map/reduce-window
  12.3 0.3 slice_reduce_fusion
  12.6 0.2 reduce-window.9
  12.8 0.1 add_bitcast_fusion
  13.0 0.0 copy-done.2
  13.0 0.1 and_reduce_fusion
  13.1 0.0 copy-done.1
  13.1 0.1 multiply_reduce_fusion
  13.2 8.1 %scatter_custom_fusion = s32[3072]{0:T(1024)S(1)} fusion(s32[2048]{0:T(1024)S(1)} %broadcast_select_fusion, s32[2048]{0:T(1024)S(1)} %iota.11, s32[]{:T(128)} %constant.10.clone.1), kind=kCustom, calls=%fused_computation.57 | custom fusion | bytes 12292
  21.3 0.6 gather_fusion
  21.9 1.1 %all-to-all-done = bf16[2,8,256,128]{3,2,0,1:T(8,128)(2,1)S(1)} async-done(((bf16[2,8,256,128]{3,2,0,1:T(8,128)(2,1)}), bf16[2,8,256,128]{3,2,0,1:T(8,128)(2,1)S(1)}, u32[]{:S(2)}, u32[]{:S(2)}) %all-to-all-start) | async-done | bytes 1048608 | tf_op jit(solution)/shard_map/all_to_all | solution.py:45
  23.0 1.1 %copy.14 = bf16[2,8,256,128]{3,0,2,1:T(2,128)(2,1)S(1)} copy(bf16[2,8,256,128]{3,2,0,1:T(8,128)(2,1)S(1)} %all-to-all-done) | data formatting | bytes 2097152 | tf_op jit(solution)/shard_map/all_to_all | solution.py:45
  24.1 1.0 %pad_bitcast_fusion = bf16[2,2049,128]{2,0,1:T(2,128)(2,1)S(1)} fusion(bf16[2,1,2048,128]{3,0,2,1:T(2,128)(2,1)S(1)} %bitcast.90), kind=kLoop, calls=%fused_computation.26 | loop fusion | bytes 2097664 | tf_op jit(solution)/shard_map/concatenate | solution.py:20
  25.1 10.4 %gather_fusion.1 = bf16[3072,2,128]{2,1,0:T(2,128)(2,1)S(1)} fusion(bf16[2,2049,128]{2,0,1:T(2,128)(2,1)S(1)} %pad_bitcast_fusion, s32[3072]{0:T(1024)S(1)} %broadcast_clamp_fusion), kind=kCustom, calls=%fused_computation.1 | custom fusion | bytes 3158016 | tf_op jit(solution)/shard_map/jit(_take)/gather | solution.py:23
  35.5 0.8 copy_select_fusion
  36.3 41.2 %all_to_all.30 = bf16[8,1,768,128]{3,2,1,0:T(8,128)(2,1)S(1)} all-to-all(bf16[8,1,768,128]{3,2,1,0:T(8,128)(2,1)S(1)} %bitcast.88), channel_id=1, replica_groups=mesh['chan'=8,'tm'=4] {'tm'}, dimensions={0} | all-to-all | bytes 3145728 | tf_op jit(solution)/shard_map/all_to_all | solution.py:50
  77.5 0.3 copy.25
  77.8 0.8 convolution_bitcast_fusion
  78.6 0.8 convolution_bitcast_fusion.1
  79.3 0.8 convolution_bitcast_fusion.2
  80.1 0.8 convolution_bitcast_fusion.3
  80.9 0.3 fusion.14
  81.2 0.3 fusion.12
  81.4 0.3 fusion.10
  81.7 0.3 fusion.8
  82.0 0.5 convert_add_fusion
  82.5 1.6 %copy.18 = f32[2,1,2,384,384]{4,3,2,1,0:T(8,128)} copy(f32[2,1,2,384,384]{4,3,0,2,1:T(8,128)S(1)} %convert_add_fusion) | data formatting | bytes 4718592 | tf_op jit(solution)/shard_map/add | solution.py:55
  (13 shorter events, 0.2 us)
Async XLA Ops:
  2.3 5.4 %copy-start = (s32[1024,1]{0,1:T(1,128)S(1)}, s32[1024,1]{0,1:T(1,128)}, u32[]{:S(2)}) copy-start(s32[1024,1]{0,1:T(1,128)} %param.4) | copy-start | bytes 12292
  2.3 6.1 %copy-start.3 = (s32[8]{0:T(128)S(1)}, s32[8]{0:T(128)}, u32[]{:S(2)}) copy-start(s32[8]{0:T(128)} %param.5) | copy-start | bytes 100
  2.3 20.7 %all-to-all-start = ((bf16[2,8,256,128]{3,2,0,1:T(8,128)(2,1)}), bf16[2,8,256,128]{3,2,0,1:T(8,128)(2,1)S(1)}, u32[]{:S(2)}, u32[]{:S(2)}) async-start(bf16[2,8,256,128]{3,2,0,1:T(8,128)(2,1)} %copy.13), calls=%async_computation | async-start | bytes 2097152 | tf_op jit(solution)/shard_map/all_to_all | solution.py:45
  7.6 5.3 %copy-start.2 = (s32[2]{0:T(128)S(1)}, s32[2]{0:T(128)}, u32[]{:S(2)}) copy-start(s32[2]{0:T(128)} %constant.36) | copy-start | bytes 28
  7.6 5.4 %copy-start.1 = (s32[2]{0:T(128)S(1)}, s32[2]{0:T(128)}, u32[]{:S(2)}) copy-start(s32[2]{0:T(128)} %constant.33) | copy-start | bytes 28
where the time goes:
time: 84.3 us; the launch traced here: 84.1 us
  blocking collectives  41.2 us (49%)
  local copies, waits for them, and re-layouts  27.2 us (32%)
  other arithmetic  5.91 us (7%)
  starting transfers between devices  5.33 us (6%)
  matrix products  3.09 us (4%)
  waiting for transfers between devices  1.08 us (1%)
    all_to_all x1, blocking collectives, shards(): lax.all_to_all(stacked, 'tm', split_axis=0, concat_axis=3, tiled=True)  41.2 us
    unnamed x12, local copies, waits for them, and re-layouts  11 us
    gather x1, local copies, waits for them, and re-layouts, compact(): picked = jnp.take(padded_voltages, rows, axis=2)  10.4 us
    all_to_all x1, starting transfers between devices, shards(): lax.all_to_all(voltages, 'chan', split_axis=1, concat_axis=2, tiled=True)  5.33 us
    dot_general x4, matrix products, gram(): jnp.einsum('...pt,...qt->...pq', stacked, stacked, preferred_element_type...  3.09 us
    another operation x2, other arithmetic  2.45 us
  transfers between devices with their start and end apart: 1, of which 1 were waited for; matrix products, arithmetic and copies ran while one was open for 17% of the time, Pallas kernels for 0%

commit v1 on v0

v1 whole, which is shorter than its diff:
```python
import jax
import jax.numpy as jnp
from jax import lax
from jax.experimental import pallas as pl
from jax.experimental.pallas import tpu as pltpu
from jax.sharding import PartitionSpec as P

SLOT = 384
LANES = 128
MESH = pl.DeviceIdType.MESH


def partner(me, step, count):
    if count & (count - 1):
        raise ValueError("axis size")
    other = me
    bit = 1
    while bit < count:
        if step & bit:
            other = other + bit - 2 * bit * (lax.div(me, bit) % 2)
        bit *= 2
    return other


def place_of_inputs(owner_ref, slots_ref, subarrays, slot):
    owner = owner_ref[...]
    rows = owner.shape[0]
    member = [(owner == slots_ref[s]).astype(jnp.float32) for s in range(subarrays)]
    stacked = jnp.concatenate(member, axis=0).astype(jnp.bfloat16)
    a = lax.broadcasted_iota(jnp.int32, (LANES, LANES), 0)
    b = lax.broadcasted_iota(jnp.int32, (LANES, LANES), 1)
    before = (a < b).astype(jnp.float32).astype(jnp.bfloat16)
    within = jnp.dot(stacked, before, preferred_element_type=jnp.float32)
    totals = jnp.dot(
        stacked, jnp.ones((LANES, LANES), jnp.bfloat16), preferred_element_type=jnp.float32
    ).astype(jnp.bfloat16)
    size = subarrays * rows
    c = lax.broadcasted_iota(jnp.int32, (size, size), 0)
    d = lax.broadcasted_iota(jnp.int32, (size, size), 1)
    earlier = ((c // rows == d // rows) & (d < c)).astype(jnp.float32).astype(jnp.bfloat16)
    rank = within + jnp.dot(earlier, totals, preferred_element_type=jnp.float32)
    half = jnp.zeros(owner.shape, jnp.float32)
    for s in range(subarrays):
        half = half + member[s] * (rank[s * rows : (s + 1) * rows] + float(s * (slot // 2)))
    high = jnp.floor(half * (1.0 / 64.0))
    low = half - high * 64.0
    e = lax.broadcasted_iota(jnp.int32, (LANES, 2 * LANES), 0)
    f = lax.broadcasted_iota(jnp.int32, (LANES, 2 * LANES), 1)
    spread = (f // 2 == e).astype(jnp.float32).astype(jnp.bfloat16)
    wide = jnp.dot(
        jnp.concatenate([high, low], axis=0).astype(jnp.bfloat16),
        spread,
        preferred_element_type=jnp.float32,
    )
    odd = (lax.broadcasted_iota(jnp.int32, (rows, 2 * LANES), 1) % 2).astype(jnp.float32)
    return 2.0 * (64.0 * wide[:rows] + wide[rows:]) + odd


def make_exchange(chans, groups, subarrays, slot, inputs, local, samples):
    held = subarrays // groups
    block = held * slot
    chan_steps = list(range(chans - 1, 0, -1))
    tm_steps = [s for s in range(groups // 2, groups)] + [s for s in range(1, groups // 2)]

    def kernel(
        volt_ref, owner_ref, slots_ref, out_ref,
        mine, arrived, pick, packed, load_sem, own_sem, csend, crecv, tsend, trecv,
    ):
        chan = lax.axis_index("chan")
        tm = lax.axis_index("tm")
        chan_peers = {s: partner(chan, s, chans) for s in chan_steps}
        tm_peers = {s: partner(tm, s, groups) for s in tm_steps}
        loads = []
        for k in range(2):
            copy = pltpu.make_async_copy(volt_ref.at[k], mine.at[k], load_sem.at[k])
            copy.start()
            loads.append(copy)
        barrier = pltpu.get_barrier_semaphore()
        for s in tm_steps:
            pl.semaphore_signal(barrier, inc=1, device_id={"tm": tm_peers[s]}, device_id_type=MESH)
        for s in chan_steps:
            pl.semaphore_signal(barrier, inc=1, device_id={"chan": chan_peers[s]}, device_id_type=MESH)
        for load in loads:
            load.wait()
        pl.semaphore_wait(barrier, len(tm_steps) + len(chan_steps))

        here = pl.ds(pl.multiple_of(chan * local, local), local)
        sent = []
        for k in range(2):
            copies = []
            for s in chan_steps:
                copy = pltpu.make_async_remote_copy(
                    src_ref=mine.at[k, chan_peers[s]],
                    dst_ref=arrived.at[k, here],
                    send_sem=csend.at[k, s],
                    recv_sem=crecv.at[k, s],
                    device_id={"chan": chan_peers[s]},
                    device_id_type=MESH,
                )
                copy.start()
                copies.append(copy)
            own = pltpu.make_async_copy(mine.at[k, chan], arrived.at[k, here], own_sem.at[k])
            own.start()
            sent.append((own, copies))

        place = place_of_inputs(owner_ref, slots_ref, subarrays, slot)
        width = 2 * LANES
        order = tm_steps + [0]
        for i, s in enumerate(order):
            holder = tm_peers[s] if s else tm
            first = (holder * block).astype(jnp.float32)
            iota = lax.broadcasted_iota(jnp.int32, (block, width), 0).astype(jnp.float32)
            for r in range(inputs // width):
                hit = iota == (place[r : r + 1] - first)
                pick[i, :, r * width : (r + 1) * width] = jnp.where(hit, 1.0, 0.0).astype(jnp.bfloat16)

        onward = []
        for k in range(2):
            own, copies = sent[k]
            own.wait()
            for copy in copies:
                copy.wait_recv()
            for i, s in enumerate(order):
                rows = jnp.dot(pick[i], arrived[k], preferred_element_type=jnp.float32)
                rows = rows.astype(jnp.bfloat16).reshape(held, slot, samples)
                if s == 0:
                    out_ref[:, k, pl.ds(tm, 1)] = rows[:, None]
                    continue
                packed[k, i] = rows
                copy = pltpu.make_async_remote_copy(
                    src_ref=packed.at[k, i],
                    dst_ref=out_ref.at[:, k, tm],
                    send_sem=tsend.at[k, s],
                    recv_sem=trecv.at[k, s],
                    device_id={"tm": tm_peers[s]},
                    device_id_type=MESH,
                )
                copy.start()
                onward.append(copy)
        for _, copies in sent:
            for copy in copies:
                copy.wait_send()
        for copy in onward:
            copy.wait()

    return pl.pallas_call(
        kernel,
        out_shape=jax.ShapeDtypeStruct((held, 2, groups, slot, samples), jnp.bfloat16),
        in_specs=[
            pl.BlockSpec(memory_space=pl.ANY),
            pl.BlockSpec(memory_space=pltpu.VMEM),
            pl.BlockSpec(memory_space=pltpu.SMEM),
        ],
        out_specs=pl.BlockSpec(memory_space=pltpu.VMEM),
        scratch_shapes=[
            pltpu.VMEM((2, chans, local, samples), jnp.bfloat16),
            pltpu.VMEM((2, inputs, samples), jnp.bfloat16),
            pltpu.VMEM((groups, block, inputs), jnp.bfloat16),
            pltpu.VMEM((2, groups - 1, held, slot, samples), jnp.bfloat16),
            pltpu.SemaphoreType.DMA((2,)),
            pltpu.SemaphoreType.DMA((2,)),
            pltpu.SemaphoreType.DMA((2, chans)),
            pltpu.SemaphoreType.DMA((2, chans)),
            pltpu.SemaphoreType.DMA((2, groups)),
            pltpu.SemaphoreType.DMA((2, groups)),
        ],
        compiler_params=pltpu.CompilerParams(
            collective_id=0, has_side_effects=True, vmem_limit_bytes=48 * 2**20
        ),
        name="exchange",
    )


def make_gram(groups, held, slot, samples):
    tile = 128
    tiles = slot // tile

    def kernel(x_ref, out_ref, stage, sems):
        copies = []
        for s in range(held):
            right = jnp.concatenate([x_ref[s, k, g] for g in range(groups) for k in range(2)], axis=-1)
            for part in range(2):
                for t in range(tiles):
                    rows = pl.ds(t * tile, tile)
                    if part == 0:
                        pieces = [x_ref[s, k, g, rows] for g in range(groups) for k in range(2)]
                    else:
                        pieces = [
                            x_ref[s, 1, g, rows] if k == 0 else -x_ref[s, 0, g, rows]
                            for g in range(groups) for k in range(2)
                        ]
                    left = jnp.concatenate(pieces, axis=-1)
                    stage[s, part, rows] = lax.dot_general(
                        left, right, (((1,), (1,)), ((), ())), preferred_element_type=jnp.float32
                    )
                    copy = pltpu.make_async_copy(
                        stage.at[s, part, rows], out_ref.at[s, 0, part, rows], sems.at[s, part, t]
                    )
                    copy.start()
                    copies.append(copy)
        for copy in copies:
            copy.wait()

    return pl.pallas_call(
        kernel,
        out_shape=jax.ShapeDtypeStruct((held, 1, 2, slot, slot), jnp.float32),
        in_specs=[pl.BlockSpec(memory_space=pltpu.VMEM)],
        out_specs=pl.BlockSpec(memory_space=pl.ANY),
        scratch_shapes=[
            pltpu.VMEM((held, 2, slot, slot), jnp.float32),
            pltpu.SemaphoreType.DMA((held, 2, tiles)),
        ],
        name="gram",
    )


def shards(voltages, assignment, slot_subarray_index):
    _, chans, local, samples = voltages.shape
    subarrays = slot_subarray_index.shape[0]
    antennas = assignment.shape[0]
    groups = lax.axis_size("tm")
    exchange = make_exchange(chans, groups, subarrays, SLOT, 2 * antennas, local, samples)
    owner = assignment.reshape(antennas // LANES, LANES)
    gathered = exchange(voltages, owner, slot_subarray_index)
    return make_gram(groups, subarrays // groups, SLOT, samples)(gathered)


def solution(mesh):
    placed = (P(None, None, "chan", "tm"), P(), P())
    return jax.shard_map(
        shards,
        mesh=mesh,
        in_specs=placed,
        out_specs=P("tm", "chan", None, None, None),
        check_vma=False,
    )
```

time: 84.3 us -> 58 us (0.69)
  the two profiles are of different devices: /device:TPU:0 before, /device:TPU:12 now
where the time goes in v1:
time: 58 us; the launch traced here: 57.8 us
  Pallas kernels  54.1 us (93%)
  local copies, waits for them, and re-layouts  3.73 us (6%)
    pallas_call x1, Pallas kernels, shards(): gathered = exchange(voltages, owner, slot_subarray_index)  49 us
    pallas_call x1, Pallas kernels, shards(): return make_gram(groups, subarrays // groups, SLOT, samples)(gathered)  5.02 us
    unnamed x8, local copies, waits for them, and re-layouts  3.73 us

profile of v1, /device:TPU:12, one launch (start us, length us, event | category | flops | bytes accessed | tf_op | source)
XLA Modules:
  0.0 57.8 jit_solution(13879234254674583682)
XLA Ops:
  0.0 0.0 copy-start.1
  0.0 1.2 %copy-done.1 = bf16[2,8,256,128]{3,2,1,0:T(8,128)(2,1)S(1)} copy-done((bf16[2,8,256,128]{3,2,1,0:T(8,128)(2,1)S(1)}, bf16[2,8,256,128]{3,2,1,0:T(8,128)(2,1)}, u32[]{:S(2)}) %copy-start.1) | copy-done | bytes 1048600
  1.2 0.0 copy-start.2
  1.2 0.7 %copy-done.2 = s32[1024,1]{0,1:T(1,128)S(1)} copy-done((s32[1024,1]{0,1:T(1,128)S(1)}, s32[1024,1]{0,1:T(1,128)}, u32[]{:S(2)}) %copy-start.2) | copy-done | bytes 4120
  1.9 0.0 copy-start.3
  1.9 0.7 %copy-done.3 = s32[8]{0:T(128)S(1)} copy-done((s32[8]{0:T(128)S(1)}, s32[8]{0:T(128)}, u32[]{:S(2)}) %copy-start.3) | copy-done | bytes 56
  2.6 49.0 %exchange.1.x_ref = bf16[2,2,4,384,128]{4,3,2,1,0:T(8,128)(2,1)S(1)} custom-call(bf16[2,8,256,128]{3,2,1,0:T(8,128)(2,1)S(1)} %copy-done.1, s32[8,128]{1,0:T(8,128)S(1)} %bitcast.1, s32[8]{0:T(128)S(1)} %copy-done.3), custom_call_target="tpu_custom_call" | custom-call | tf_op jit(solution)/shard_map/exchange/pallas_call | solution.py:224
  51.6 0.0 copy-start
  51.6 1.2 %copy-done = bf16[2,2,4,384,128]{4,3,2,1,0:T(8,128)(2,1)} copy-done((bf16[2,2,4,384,128]{4,3,2,1,0:T(8,128)(2,1)}, bf16[2,2,4,384,128]{4,3,2,1,0:T(8,128)(2,1)S(1)}, u32[]{:S(2)}) %copy-start) | copy-done | bytes 1572888
  52.8 5.0 %gram.1 = f32[2,1,2,384,384]{4,3,2,1,0:T(8,128)} custom-call(bf16[2,2,4,384,128]{4,3,2,1,0:T(8,128)(2,1)} %copy-done), custom_call_target="tpu_custom_call" | custom-call | tf_op jit(solution)/shard_map/gram/pallas_call | solution.py:225
Async XLA Ops:
  0.0 1.2 %copy-start.1 = (bf16[2,8,256,128]{3,2,1,0:T(8,128)(2,1)S(1)}, bf16[2,8,256,128]{3,2,1,0:T(8,128)(2,1)}, u32[]{:S(2)}) copy-start(bf16[2,8,256,128]{3,2,1,0:T(8,128)(2,1)} %volt_ref.1) | copy-start | bytes 3145732
  1.2 0.7 %copy-start.2 = (s32[1024,1]{0,1:T(1,128)S(1)}, s32[1024,1]{0,1:T(1,128)}, u32[]{:S(2)}) copy-start(s32[1024,1]{0,1:T(1,128)} %param.4) | copy-start | bytes 12292
  1.9 0.7 %copy-start.3 = (s32[8]{0:T(128)S(1)}, s32[8]{0:T(128)}, u32[]{:S(2)}) copy-start(s32[8]{0:T(128)} %slots_ref.1) | copy-start | bytes 100
  51.6 1.2 %copy-start = (bf16[2,2,4,384,128]{4,3,2,1,0:T(8,128)(2,1)}, bf16[2,2,4,384,128]{4,3,2,1,0:T(8,128)(2,1)S(1)}, u32[]{:S(2)}) copy-start(bf16[2,2,4,384,128]{4,3,2,1,0:T(8,128)(2,1)S(1)} %exchange.1.x_ref) | copy-start | bytes 4718596

commit v2 on v1

v2 whole, which is shorter than its diff:
```python
import jax
import jax.numpy as jnp
from jax import lax
from jax.experimental import pallas as pl
from jax.experimental.pallas import tpu as pltpu
from jax.sharding import PartitionSpec as P

SLOT = 384
LANES = 128
MESH = pl.DeviceIdType.MESH


def partner(me, step, count):
    if count & (count - 1):
        raise ValueError("axis size")
    other = me
    bit = 1
    while bit < count:
        if step & bit:
            other = other + bit - 2 * bit * (lax.div(me, bit) % 2)
        bit *= 2
    return other


def place_of_inputs(owner_ref, slots_ref, subarrays, slot):
    owner = owner_ref[...]
    rows = owner.shape[0]
    member = [(owner == slots_ref[s]).astype(jnp.float32) for s in range(subarrays)]
    stacked = jnp.concatenate(member, axis=0).astype(jnp.bfloat16)
    a = lax.broadcasted_iota(jnp.int32, (LANES, LANES), 0)
    b = lax.broadcasted_iota(jnp.int32, (LANES, LANES), 1)
    before = (a < b).astype(jnp.float32).astype(jnp.bfloat16)
    within = jnp.dot(stacked, before, preferred_element_type=jnp.float32)
    totals = jnp.dot(
        stacked, jnp.ones((LANES, LANES), jnp.bfloat16), preferred_element_type=jnp.float32
    ).astype(jnp.bfloat16)
    size = subarrays * rows
    c = lax.broadcasted_iota(jnp.int32, (size, size), 0)
    d = lax.broadcasted_iota(jnp.int32, (size, size), 1)
    earlier = ((c // rows == d // rows) & (d < c)).astype(jnp.float32).astype(jnp.bfloat16)
    rank = within + jnp.dot(earlier, totals, preferred_element_type=jnp.float32)
    half = jnp.zeros(owner.shape, jnp.float32)
    for s in range(subarrays):
        half = half + member[s] * (rank[s * rows : (s + 1) * rows] + float(s * (slot // 2)))
    high = jnp.floor(half * (1.0 / 64.0))
    low = half - high * 64.0
    e = lax.broadcasted_iota(jnp.int32, (LANES, 2 * LANES), 0)
    f = lax.broadcasted_iota(jnp.int32, (LANES, 2 * LANES), 1)
    spread = (f // 2 == e).astype(jnp.float32).astype(jnp.bfloat16)
    wide = jnp.dot(
        jnp.concatenate([high, low], axis=0).astype(jnp.bfloat16),
        spread,
        preferred_element_type=jnp.float32,
    )
    odd = (lax.broadcasted_iota(jnp.int32, (rows, 2 * LANES), 1) % 2).astype(jnp.float32)
    return 2.0 * (64.0 * wide[:rows] + wide[rows:]) + odd


def flip(me, mask, count):
    out = me * 0
    bit = 1
    while bit < count:
        out = out + bit * ((lax.div(me, bit) + lax.div(mask, bit)) % 2)
        bit *= 2
    return out


def line_order(tm, groups):
    if groups != 4:
        masks = [tm * 0 + s for s in range(1, groups)]
        return masks, masks
    inner = lax.div(tm + 1, 2) % 2
    return [1 + inner, 2 + inner, 3 - 2 * inner], [tm * 0 + 1, 2 + inner, 3 - inner]


def make_correlator(chans, groups, subarrays, slot, antennas, local, samples):
    held = subarrays // groups
    block = held * slot
    inputs = 2 * antennas
    width = 2 * LANES
    chan_steps = list(range(chans - 1, 0, -1))

    def kernel(
        volt_hbm, owner_hbm, slots_hbm, out_ref,
        mine, arrived, pick, packed, taken, owner_ref, slots_ref,
        load_sem, own_sem, csend, crecv, tsend, trecv,
    ):
        chan = lax.axis_index("chan")
        tm = lax.axis_index("tm")
        chan_peers = {s: partner(chan, s, chans) for s in chan_steps}
        send_masks, recv_masks = line_order(tm, groups)
        tm_peers = [flip(tm, m, groups) for m in send_masks]

        loads = [
            pltpu.make_async_copy(volt_hbm.at[0], mine.at[0], load_sem.at[0]),
            pltpu.make_async_copy(slots_hbm, slots_ref, load_sem.at[2]),
            pltpu.make_async_copy(owner_hbm, owner_ref, load_sem.at[3]),
            pltpu.make_async_copy(volt_hbm.at[1], mine.at[1], load_sem.at[1]),
        ]
        for load in loads:
            load.start()
        barrier = pltpu.get_barrier_semaphore()
        for peer in tm_peers:
            pl.semaphore_signal(barrier, inc=1, device_id={"tm": peer}, device_id_type=MESH)
        for s in chan_steps:
            pl.semaphore_signal(barrier, inc=1, device_id={"chan": chan_peers[s]}, device_id_type=MESH)
        for load in loads:
            load.wait()
        pl.semaphore_wait(barrier, len(tm_peers) + len(chan_steps))

        here = pl.ds(pl.multiple_of(chan * local, local), local)

        def swap_channels(k):
            copies = []
            for s in chan_steps:
                copy = pltpu.make_async_remote_copy(
                    src_ref=mine.at[k, chan_peers[s]],
                    dst_ref=arrived.at[k, here],
                    send_sem=csend.at[k, s],
                    recv_sem=crecv.at[k, s],
                    device_id={"chan": chan_peers[s]},
                    device_id_type=MESH,
                )
                copy.start()
                copies.append(copy)
            own = pltpu.make_async_copy(mine.at[k, chan], arrived.at[k, here], own_sem.at[k])
            own.start()
            return own, copies

        swaps = [swap_channels(0), None]

        place = place_of_inputs(owner_ref, slots_ref, subarrays, slot)
        iota = lax.broadcasted_iota(jnp.int32, (block, width), 0).astype(jnp.float32)
        for i, holder in enumerate(tm_peers + [tm]):
            first = (holder * block).astype(jnp.float32)
            for r in range(inputs // width):
                hit = iota == (place[r : r + 1] - first)
                pick[i, :, r * width : (r + 1) * width] = jnp.where(hit, 1.0, 0.0).astype(jnp.bfloat16)

        onward = []
        for k in range(2):
            own, copies = swaps[k]
            own.wait()
            for copy in copies:
                copy.wait_recv()
            if k == 0:
                swaps[1] = swap_channels(1)
            for i, peer in enumerate(tm_peers + [tm]):
                rows = jnp.dot(pick[i], arrived[k], preferred_element_type=jnp.float32)
                rows = rows.astype(jnp.bfloat16).reshape(held, slot, samples)
                if i == groups - 1:
                    taken[:, k, pl.ds(tm, 1)] = rows[:, None]
                    continue
                packed[k, i] = rows
                copy = pltpu.make_async_remote_copy(
                    src_ref=packed.at[k, i],
                    dst_ref=taken.at[:, k, tm],
                    send_sem=tsend.at[k, send_masks[i]],
                    recv_sem=trecv.at[k, send_masks[i]],
                    device_id={"tm": peer},
                    device_id_type=MESH,
                )
                copy.start()
                onward.append(copy)

        def add_block(group, fresh):
            for s in range(held):
                re = taken[s, 0, group]
                im = taken[s, 1, group]
                right = jnp.concatenate([re, im], axis=-1)
                for part, left in ((0, right), (1, jnp.concatenate([im, -re], axis=-1))):
                    term = lax.dot_general(
                        left, right, (((1,), (1,)), ((), ())), preferred_element_type=jnp.float32
                    )
                    if fresh:
                        out_ref[s, 0, part] = term
                    else:
                        out_ref[s, 0, part] += term

        add_block(tm, True)
        for mask in recv_masks:
            peer = flip(tm, mask, groups)
            for k in range(2):
                pltpu.make_async_remote_copy(
                    src_ref=packed.at[k, 0],
                    dst_ref=taken.at[:, k, peer],
                    send_sem=tsend.at[k, mask],
                    recv_sem=trecv.at[k, mask],
                    device_id={"tm": peer},
                    device_id_type=MESH,
                ).wait_recv()
            add_block(peer, False)
        for _, copies in swaps:
            for copy in copies:
                copy.wait_send()
        for copy in onward:
            copy.wait_send()

    return pl.pallas_call(
        kernel,
        out_shape=jax.ShapeDtypeStruct((held, 1, 2, slot, slot), jnp.float32),
        in_specs=[pl.BlockSpec(memory_space=pltpu.HBM)] * 3,
        out_specs=pl.BlockSpec(memory_space=pltpu.VMEM),
        scratch_shapes=[
            pltpu.VMEM((2, chans, local, samples), jnp.bfloat16),
            pltpu.VMEM((2, inputs, samples), jnp.bfloat16),
            pltpu.VMEM((groups, block, inputs), jnp.bfloat16),
            pltpu.VMEM((2, groups - 1, held, slot, samples), jnp.bfloat16),
            pltpu.VMEM((held, 2, groups, slot, samples), jnp.bfloat16),
            pltpu.VMEM((antennas // LANES, LANES), jnp.int32),
            pltpu.SMEM((subarrays,), jnp.int32),
            pltpu.SemaphoreType.DMA((4,)),
            pltpu.SemaphoreType.DMA((2,)),
            pltpu.SemaphoreType.DMA((2, chans)),
            pltpu.SemaphoreType.DMA((2, chans)),
            pltpu.SemaphoreType.DMA((2, groups)),
            pltpu.SemaphoreType.DMA((2, groups)),
        ],
        compiler_params=pltpu.CompilerParams(
            collective_id=0, has_side_effects=True, vmem_limit_bytes=61 * 2**20
        ),
        name="correlate",
    )


def shards(voltages, assignment, slot_subarray_index):
    _, chans, local, samples = voltages.shape
    subarrays = slot_subarray_index.shape[0]
    antennas = assignment.shape[0]
    groups = lax.axis_size("tm")
    correlate = make_correlator(chans, groups, subarrays, SLOT, antennas, local, samples)
    return correlate(voltages, assignment.reshape(antennas // LANES, LANES), slot_subarray_index)


def solution(mesh):
    placed = (P(None, None, "chan", "tm"), P(), P())
    return jax.shard_map(
        shards,
        mesh=mesh,
        in_specs=placed,
        out_specs=P("tm", "chan", None, None, None),
        check_vma=False,
    )
```

time: 58 us -> 54 us (0.931)
  Pallas kernels: 54.1 us -> 50.6 us
    pallas_call x2 -> x1, Pallas kernels: 54.1 us -> 50.6 us  [shards(): correlate(voltages, assignment.reshape(antennas // LANES, LANES), slot_su...]
    unnamed x8 -> x1, local copies, waits for them, and re-layouts: 3.73 us -> 3.23 us
where the time goes in v2:
time: 54 us; the launch traced here: 53.9 us
  Pallas kernels  50.6 us (94%)
  local copies, waits for them, and re-layouts  3.23 us (6%)
    pallas_call x1, Pallas kernels, shards(): correlate(voltages, assignment.reshape(antennas // LANES, LANES), slot_su...  50.6 us
    unnamed x1, local copies, waits for them, and re-layouts  3.23 us

profile of v2, /device:TPU:12, one launch (start us, length us, event | category | flops | bytes accessed | tf_op | source)
XLA Modules:
  0.0 53.9 jit_solution(4777913754614738268)
XLA Ops:
  0.0 50.6 %correlate.1 = f32[2,1,2,384,384]{4,3,2,1,0:T(8,128)} custom-call(bf16[2,8,256,128]{3,2,1,0:T(8,128)(2,1)} %volt_hbm.1, s32[8,128]{1,0:T(8,128)} %bitcast.1, s32[8]{0:T(128)} %slots_hbm.1), custom_call_target="tpu_custom_call" | custom-call | tf_op jit(solution)/shard_map/correlate/pallas_call | solution.py:232
  50.6 3.2 %copy.5 = f32[2,1,2,384,384]{4,3,2,1,0:T(8,128)} copy(f32[2,1,2,384,384]{4,3,2,1,0:T(8,128)} %correlate.1) | data formatting | bytes 4718592

commit v3 on v2

--- a/solution.py
+++ b/solution.py
@@ -217,7 +217,7 @@
             pltpu.SemaphoreType.DMA((2, groups)),
         ],
         compiler_params=pltpu.CompilerParams(
-            collective_id=0, has_side_effects=True, vmem_limit_bytes=61 * 2**20
+            collective_id=0, has_side_effects=True, vmem_limit_bytes=48 * 2**20
         ),
         name="correlate",
     )
@@ -229,7 +229,9 @@
     antennas = assignment.shape[0]
     groups = lax.axis_size("tm")
     correlate = make_correlator(chans, groups, subarrays, SLOT, antennas, local, samples)
-    return correlate(voltages, assignment.reshape(antennas // LANES, LANES), slot_subarray_index)
+    owner = assignment.reshape(antennas // LANES, LANES)
+    operands = [pltpu.with_memory_space_constraint(x, pltpu.HBM) for x in (voltages, owner, slot_subarray_index)]
+    return correlate(*operands)
 
 
 def solution(mesh):

time: 54 us -> 50.8 us (0.941)
  local copies, waits for them, and re-layouts: 3.23 us -> 1.41 us
  Pallas kernels: 50.6 us -> 49.3 us
    unnamed x1, local copies, waits for them, and re-layouts: 3.23 us -> 1.41 us
    pallas_call x1, Pallas kernels: 50.6 us -> 49.3 us  [shards(): return correlate(*operands)]
where the time goes in v3:
time: 50.8 us; the launch traced here: 50.7 us
  Pallas kernels  49.3 us (97%)
  local copies, waits for them, and re-layouts  1.41 us (3%)
    pallas_call x1, Pallas kernels, shards(): return correlate(*operands)  49.3 us
    unnamed x1, local copies, waits for them, and re-layouts  1.41 us

profile of v3, /device:TPU:12, one launch (start us, length us, event | category | flops | bytes accessed | tf_op | source)
XLA Modules:
  0.0 50.7 jit_solution(2374740681576371386)
XLA Ops:
  0.0 49.3 %correlate.1 = f32[2,1,2,384,384]{4,3,2,1,0:T(8,128)S(1)} custom-call(bf16[2,8,256,128]{3,2,1,0:T(8,128)(2,1)} %volt_hbm.1, s32[8,128]{1,0:T(8,128)} %bitcast.1, s32[8]{0:T(128)} %slots_hbm.1), custom_call_target="tpu_custom_call" | custom-call | tf_op jit(solution)/shard_map/correlate/pallas_call | solution.py:234
  49.3 1.4 %copy.5 = f32[2,1,2,384,384]{4,3,2,1,0:T(8,128)} copy(f32[2,1,2,384,384]{4,3,2,1,0:T(8,128)S(1)} %correlate.1) | data formatting | bytes 4718592

commit v4 on v3

--- a/solution.py
+++ b/solution.py
@@ -146,50 +146,53 @@
             if k == 0:
                 swaps[1] = swap_channels(1)
             for i, peer in enumerate(tm_peers + [tm]):
-                rows = jnp.dot(pick[i], arrived[k], preferred_element_type=jnp.float32)
-                rows = rows.astype(jnp.bfloat16).reshape(held, slot, samples)
-                if i == groups - 1:
-                    taken[:, k, pl.ds(tm, 1)] = rows[:, None]
-                    continue
-                packed[k, i] = rows
-                copy = pltpu.make_async_remote_copy(
-                    src_ref=packed.at[k, i],
-                    dst_ref=taken.at[:, k, tm],
-                    send_sem=tsend.at[k, send_masks[i]],
-                    recv_sem=trecv.at[k, send_masks[i]],
-                    device_id={"tm": peer},
-                    device_id_type=MESH,
+                for h in range(held):
+                    rows = jnp.dot(
+                        pick[i, h * slot : (h + 1) * slot], arrived[k], preferred_element_type=jnp.float32
+                    ).astype(jnp.bfloat16)
+                    if i == groups - 1:
+                        taken[h, k, tm] = rows
+                        continue
+                    packed[k, i, h] = rows
+                    copy = pltpu.make_async_remote_copy(
+                        src_ref=packed.at[k, i, h],
+                        dst_ref=taken.at[h, k, tm],
+                        send_sem=tsend.at[k, h, send_masks[i]],
+                        recv_sem=trecv.at[k, h, send_masks[i]],
+                        device_id={"tm": peer},
+                        device_id_type=MESH,
+                    )
+                    copy.start()
+                    onward.append(copy)
+
+        def add_block(group, s, fresh):
+            re = taken[s, 0, group]
+            im = taken[s, 1, group]
+            right = jnp.concatenate([re, im], axis=-1)
+            for part, left in ((0, right), (1, jnp.concatenate([im, -re], axis=-1))):
+                term = lax.dot_general(
+                    left, right, (((1,), (1,)), ((), ())), preferred_element_type=jnp.float32
                 )
-                copy.start()
-                onward.append(copy)
-
-        def add_block(group, fresh):
-            for s in range(held):
-                re = taken[s, 0, group]
-                im = taken[s, 1, group]
-                right = jnp.concatenate([re, im], axis=-1)
-                for part, left in ((0, right), (1, jnp.concatenate([im, -re], axis=-1))):
-                    term = lax.dot_general(
-                        left, right, (((1,), (1,)), ((), ())), preferred_element_type=jnp.float32
-                    )
-                    if fresh:
-                        out_ref[s, 0, part] = term
-                    else:
-                        out_ref[s, 0, part] += term
-
-        add_block(tm, True)
+                if fresh:
+                    out_ref[s, 0, part] = term
+                else:
+                    out_ref[s, 0, part] += term
+
+        for h in range(held):
+            add_block(tm, h, True)
         for mask in recv_masks:
             peer = flip(tm, mask, groups)
-            for k in range(2):
-                pltpu.make_async_remote_copy(
-                    src_ref=packed.at[k, 0],
-                    dst_ref=taken.at[:, k, peer],
-                    send_sem=tsend.at[k, mask],
-                    recv_sem=trecv.at[k, mask],
-                    device_id={"tm": peer},
-                    device_id_type=MESH,
-                ).wait_recv()
-            add_block(peer, False)
+            for h in range(held):
+                for k in range(2):
+                    pltpu.make_async_remote_copy(
+                        src_ref=packed.at[k, 0, h],
+                        dst_ref=taken.at[h, k, peer],
+                        send_sem=tsend.at[k, h, mask],
+                        recv_sem=trecv.at[k, h, mask],
+                        device_id={"tm": peer},
+                        device_id_type=MESH,
+                    ).wait_recv()
+                add_block(peer, h, False)
         for _, copies in swaps:
             for copy in copies:
                 copy.wait_send()
@@ -213,8 +216,8 @@
             pltpu.SemaphoreType.DMA((2,)),
             pltpu.SemaphoreType.DMA((2, chans)),
             pltpu.SemaphoreType.DMA((2, chans)),
-            pltpu.SemaphoreType.DMA((2, groups)),
-            pltpu.SemaphoreType.DMA((2, groups)),
+            pltpu.SemaphoreType.DMA((2, held, groups)),
+            pltpu.SemaphoreType.DMA((2, held, groups)),
         ],
         compiler_params=pltpu.CompilerParams(
             collective_id=0, has_side_effects=True, vmem_limit_bytes=48 * 2**20

time: 50.8 us -> 50.2 us (0.988)
  Pallas kernels: 49.3 us -> 48.6 us
    pallas_call x1, Pallas kernels: 49.3 us -> 48.6 us  [shards(): return correlate(*operands)]
where the time goes in v4:
time: 50.2 us; the launch traced here: 50 us
  Pallas kernels  48.6 us (97%)
  local copies, waits for them, and re-layouts  1.41 us (3%)
    pallas_call x1, Pallas kernels, shards(): return correlate(*operands)  48.6 us
    unnamed x1, local copies, waits for them, and re-layouts  1.41 us

profile of v4, /device:TPU:12, one launch (start us, length us, event | category | flops | bytes accessed | tf_op | source)
XLA Modules:
  0.0 50.0 jit_solution(3569396049961859654)
XLA Ops:
  0.0 48.6 %correlate.1 = f32[2,1,2,384,384]{4,3,2,1,0:T(8,128)S(1)} custom-call(bf16[2,8,256,128]{3,2,1,0:T(8,128)(2,1)} %volt_hbm.1, s32[8,128]{1,0:T(8,128)} %bitcast.1, s32[8]{0:T(128)} %slots_hbm.1), custom_call_target="tpu_custom_call" | custom-call | tf_op jit(solution)/shard_map/correlate/pallas_call | solution.py:237
  48.6 1.4 %copy.5 = f32[2,1,2,384,384]{4,3,2,1,0:T(8,128)} copy(f32[2,1,2,384,384]{4,3,2,1,0:T(8,128)S(1)} %correlate.1) | data formatting | bytes 4718592
